TPU v7x, 32 devices: a 4x4x1 block of a 4x4x8 slice. The times are simulated.
32 devices in a mesh: frag: 1 (over z), dev: 32 (over y, x, core).
Axes of the slice: x: 4, y: 4, z: 1, core: 2. Of those that a mesh axis runs over, the one named last changes fastest.
The devices are a block of a 4x4x8 slice.
Arguments:
- ao_ints: bfloat16 [160, 160, 160, 160], P(('frag', 'dev'))
- c_occ: bfloat16 [160, 32], P('frag')
- c_vir: bfloat16 [160, 104], P('frag')
Outputs:
- output 1: float32 [104, 104, 1024], P('frag', None, 'dev')
- output 2: float32 [32, 104, 3328], P('frag', None, 'dev')
All inputs are finite; a program needn't handle non-finite values.
Results may differ from a plain program's by a relative error of at most 0.001.
Values are sent between devices in bfloat16 or wider.
A program may use at most 768 MiB of HBM per device.

v0:
```python
import jax
import jax.numpy as jnp
from jax import lax
from jax.sharding import PartitionSpec as P


def solution(mesh):
    def local_part(ao_rows, c_occ, c_vir):
        n_rows = ao_rows.shape[0]
        n_ao = ao_rows.shape[1]
        n_occ = c_occ.shape[1]
        n_vir = c_vir.shape[1]
        quarter = jnp.einsum('pqrs,rx->pqsx', ao_rows, c_occ, preferred_element_type=jnp.float32).astype(jnp.bfloat16)
        half_oo = jnp.einsum('pqsx,sj->pqxj', quarter, c_occ, preferred_element_type=jnp.float32).astype(jnp.bfloat16)
        half_ov = jnp.einsum('pqsx,sb->pqxb', quarter, c_vir, preferred_element_type=jnp.float32).astype(jnp.bfloat16)
        half_oo = half_oo.reshape(n_rows, n_ao, n_occ * n_occ)
        half_ov = half_ov.reshape(n_rows, n_ao, n_occ * n_vir)
        full_oo = lax.all_to_all(half_oo, 'dev', 2, 0, tiled=True)
        full_ov = lax.all_to_all(half_ov, 'dev', 2, 0, tiled=True)
        mid_oo = jnp.einsum('qrn,rc->qcn', full_oo, c_vir, preferred_element_type=jnp.float32).astype(jnp.bfloat16)
        mid_ov = jnp.einsum('qrn,rb->qbn', full_ov, c_vir, preferred_element_type=jnp.float32).astype(jnp.bfloat16)
        v_abij = jnp.einsum('pa,pbm->abm', c_vir, mid_oo, preferred_element_type=jnp.float32)
        v_iajb = jnp.einsum('pi,pam->iam', c_occ, mid_ov, preferred_element_type=jnp.float32)
        return v_abij, v_iajb

    return jax.shard_map(local_part, mesh=mesh,
                         in_specs=(P(('frag', 'dev')), P('frag'), P('frag')),
                         out_specs=(P('frag', None, 'dev'), P('frag', None, 'dev')),
                         check_vma=False)
```

profile of v0, /device:TPU:103, one launch (start us, length us, event | category | flops | bytes accessed | tf_op | source)
XLA Modules:
  0.0 264.7 jit_solution(11811838062253945587)
XLA Ops:
  0.6 0.0 copy-start
  0.7 30.2 %convolution_convert_fusion = bf16[5,160,160,32]{2,3,1,0:T(8,128)(2,1)} fusion(bf16[5,160,160,160]{3,2,1,0:T(8,128)(2,1)} %param.3, bf16[160,32]{0,1:T(8,128)(2,1)} %param.4), kind=kOutput, calls=%fused_computation | convolution fusion | flops 1314816000 | bytes 49162240 | tf_op jit(solution)/shard_map/pqrs,rx->pqsx/dot_general | solution.py:13
  30.8 11.0 %convolution_convert_fusion.2 = bf16[5,160,32,32]{3,2,1,0:T(8,128)(2,1)} fusion(bf16[5,160,160,32]{2,3,1,0:T(8,128)(2,1)} %convolution_convert_fusion, bf16[160,32]{0,1:T(8,128)(2,1)S(1)} %copy-done.1), kind=kOutput, calls=%fused_computation.2 | convolution fusion | flops 262963200 | bytes 9840640 | tf_op jit(solution)/shard_map/pqsx,sj->pqxj/dot_general | solution.py:14
  41.8 13.4 %copy.31 = bf16[5,160,32,32]{1,0,3,2:T(8,128)(2,1)} copy(bf16[5,160,32,32]{3,2,1,0:T(8,128)(2,1)} %convolution_convert_fusion.2) | data formatting | bytes 3276800 | tf_op jit(solution)/shard_map/reshape | solution.py:16
  55.2 7.9 %reshape.16 = bf16[32,2,12800]{2,1,0:T(2,128)(2,1)} reshape(bf16[1024,5,160]{2,1,0:T(8,128)(2,1)} %bitcast.57) | data formatting | bytes 3276800
  63.1 8.0 %all-to-all-start = ((bf16[32,2,12800]{2,1,0:T(2,128)(2,1)}), bf16[32,2,12800]{2,1,0:T(2,128)(2,1)S(1)}, u32[]{:S(2)}, u32[]{:S(2)}) async-start(bf16[32,2,12800]{2,1,0:T(2,128)(2,1)} %reshape.16), calls=%async_computation | async-start | bytes 3276800 | tf_op jit(solution)/shard_map/all_to_all | solution.py:18
  71.1 10.9 %convolution_convert_fusion.1 = bf16[5,160,32,104]{3,2,1,0:T(8,128)(2,1)} fusion(bf16[5,160,160,32]{2,3,1,0:T(8,128)(2,1)} %convolution_convert_fusion, bf16[160,104]{1,0:T(8,128)(2,1)S(1)} %copy-done), kind=kOutput, calls=%fused_computation.1 | convolution fusion | flops 854630400 | bytes 13550080 | tf_op jit(solution)/shard_map/pqsx,sb->pqxb/dot_general | solution.py:15
  82.0 15.7 %copy.33 = bf16[5,160,32,104]{1,0,3,2:T(8,128)(2,1)} copy(bf16[5,160,32,104]{3,2,1,0:T(8,128)(2,1)} %convolution_convert_fusion.1) | data formatting | bytes 10649600 | tf_op jit(solution)/shard_map/reshape | solution.py:17
  97.7 26.9 %reshape.18 = bf16[32,2,41600]{2,1,0:T(2,128)(2,1)} reshape(bf16[3328,5,160]{2,1,0:T(8,128)(2,1)} %bitcast.53) | data formatting | bytes 10649600
  124.6 0.0 all-to-all-done
  124.6 6.3 %all-to-all-start.1 = ((bf16[32,2,41600]{2,1,0:T(2,128)(2,1)}), bf16[32,2,41600]{2,1,0:T(2,128)(2,1)}, u32[]{:S(2)}, u32[]{:S(2)}) async-start(bf16[32,2,41600]{2,1,0:T(2,128)(2,1)} %reshape.18), calls=%async_computation.1 | async-start | bytes 10649600 | tf_op jit(solution)/shard_map/all_to_all | solution.py:19
  130.9 5.4 %reshape.17 = bf16[1024,5,160]{2,1,0:T(8,128)(2,1)} reshape(bf16[32,2,12800]{2,1,0:T(2,128)(2,1)S(1)} %all-to-all-done) | data formatting | bytes 3276800
  136.4 3.1 %copy.21 = bf16[32,5,160,32]{2,3,1,0:T(8,128)(2,1)S(1)} copy(bf16[32,5,160,32]{2,1,3,0:T(8,128)(2,1)} %bitcast.56) | data formatting | bytes 3276800 | tf_op jit(solution)/shard_map/all_to_all | solution.py:18
  139.5 0.8 fusion
  140.3 3.0 %copy.22 = bf16[160,104,32]{0,2,1:T(8,128)(2,1)S(1)} copy(bf16[160,104,32]{1,2,0:T(8,128)(2,1)S(1)} %fusion) | data formatting | bytes 2129920 | tf_op jit(solution)/shard_map/convert_element_type | solution.py:20
  143.3 0.6 convolution_bitcast_fusion.1
  143.9 2.0 copy.27
  145.9 55.5 %all-to-all-done.1 = bf16[32,2,41600]{2,1,0:T(2,128)(2,1)} async-done(((bf16[32,2,41600]{2,1,0:T(2,128)(2,1)}), bf16[32,2,41600]{2,1,0:T(2,128)(2,1)}, u32[]{:S(2)}, u32[]{:S(2)}) %all-to-all-start.1) | async-done | bytes 5324832 | tf_op jit(solution)/shard_map/all_to_all | solution.py:19
  201.4 27.7 %reshape.19 = bf16[3328,5,160]{2,1,0:T(8,128)(2,1)} reshape(bf16[32,2,41600]{2,1,0:T(2,128)(2,1)} %all-to-all-done.1) | data formatting | bytes 10649600
  229.1 15.5 %copy.25 = bf16[32,5,160,104]{3,2,1,0:T(8,128)(2,1)} copy(bf16[32,5,160,104]{2,1,3,0:T(8,128)(2,1)} %bitcast.54) | data formatting | bytes 10649600 | tf_op jit(solution)/shard_map/all_to_all | solution.py:19
  244.6 7.6 %convert_bitcast_fusion = bf16[160,104,104]{1,2,0:T(8,128)(2,1)} fusion(bf16[160,160,104]{2,1,0:T(8,128)(2,1)} %bitcast.55, bf16[160,104]{1,0:T(8,128)(2,1)S(1)} %copy-done), kind=kOutput, calls=%fused_computation.3 | convolution fusion | flops 555509760 | bytes 8819200 | tf_op jit(solution)/shard_map/qrn,rb->qbn/dot_general | solution.py:21
  252.3 7.4 %copy.26 = bf16[160,104,104]{2,0,1:T(8,128)(2,1)} copy(bf16[160,104,104]{1,2,0:T(8,128)(2,1)} %convert_bitcast_fusion) | data formatting | bytes 6922240 | tf_op jit(solution)/shard_map/convert_element_type | solution.py:21
  259.6 2.9 %convolution_bitcast_fusion = f32[32,104,104]{2,0,1:T(8,128)S(1)} fusion(bf16[160,104,104]{2,0,1:T(8,128)(2,1)} %copy.26, bf16[160,32]{0,1:T(8,128)(2,1)S(1)} %copy-done.1), kind=kOutput, calls=%fused_computation.5 | convolution fusion | flops 110755840 | bytes 4855808 | tf_op jit(solution)/shard_map/pi,pam->iam/dot_general | solution.py:23
  262.5 2.2 copy.28
  (3 shorter events, 0.0 us)
Async XLA Ops:
  0.6 70.5 %copy-start = (bf16[160,104]{1,0:T(8,128)(2,1)S(1)}, bf16[160,104]{1,0:T(8,128)(2,1)}, u32[]{:S(2)}) copy-start(bf16[160,104]{1,0:T(8,128)(2,1)} %param.5) | copy-start | bytes 99844
  0.6 30.2 %copy-start.1 = (bf16[160,32]{0,1:T(8,128)(2,1)S(1)}, bf16[160,32]{0,1:T(8,128)(2,1)}, u32[]{:S(2)}) copy-start(bf16[160,32]{0,1:T(8,128)(2,1)} %param.4) | copy-start | bytes 30724
  63.1 61.5 %all-to-all-start = ((bf16[32,2,12800]{2,1,0:T(2,128)(2,1)}), bf16[32,2,12800]{2,1,0:T(2,128)(2,1)S(1)}, u32[]{:S(2)}, u32[]{:S(2)}) async-start(bf16[32,2,12800]{2,1,0:T(2,128)(2,1)} %reshape.16), calls=%async_computation | async-start | bytes 3276800 | tf_op jit(solution)/shard_map/all_to_all | solution.py:18
  124.6 76.8 %all-to-all-start.1 = ((bf16[32,2,41600]{2,1,0:T(2,128)(2,1)}), bf16[32,2,41600]{2,1,0:T(2,128)(2,1)}, u32[]{:S(2)}, u32[]{:S(2)}) async-start(bf16[32,2,41600]{2,1,0:T(2,128)(2,1)} %reshape.18), calls=%async_computation.1 | async-start | bytes 10649600 | tf_op jit(solution)/shard_map/all_to_all | solution.py:19
where the time goes:
time: 267 us; the launch traced here: 265 us
  local copies, waits for them, and re-layouts  130 us (49%)
  matrix products  64 us (24%)
  waiting for transfers between devices  55.5 us (21%)
  starting transfers between devices  14.3 us (5%)
    unnamed x10, local copies, waits for them, and re-layouts  72.2 us
    all_to_all x1, waiting for transfers between devices, local_part(): full_ov = lax.all_to_all(half_ov, 'dev', 2, 0, tiled=True)  55.5 us
    dot_general x1, matrix products, local_part(): jnp.einsum('pqrs,rx->pqsx', ao_rows, c_occ, preferred_element_type=jnp.fl...  30.2 us
    reshape x1, local copies, waits for them, and re-layouts, local_part(): half_ov = half_ov.reshape(n_rows, n_ao, n_occ * n_vir)  15.7 us
    all_to_all x1, local copies, waits for them, and re-layouts, local_part(): full_ov = lax.all_to_all(half_ov, 'dev', 2, 0, tiled=True)  15.5 us
    reshape x1, local copies, waits for them, and re-layouts, local_part(): half_oo = half_oo.reshape(n_rows, n_ao, n_occ * n_occ)  13.4 us
    dot_general x1, matrix products, local_part(): jnp.einsum('pqsx,sj->pqxj', quarter, c_occ, preferred_element_type=jnp.fl...  11 us
    dot_general x1, matrix products, local_part(): jnp.einsum('pqsx,sb->pqxb', quarter, c_vir, preferred_element_type=jnp.fl...  10.9 us
  transfers between devices with their start and end apart: 2, of which 1 were waited for; matrix products, arithmetic and copies ran while one was open for 26% of the time, Pallas kernels for 0%

commit v1 on v0

v1 whole, which is shorter than its diff:
```python
import functools

import jax
import jax.numpy as jnp
from jax import lax
from jax.experimental import pallas as pl
from jax.experimental.pallas import tpu as pltpu
from jax.sharding import PartitionSpec as P

F32 = jnp.float32
BF16 = jnp.bfloat16
LANES = 128
TILE = 16
GROUP = 8


def _dot(lhs, rhs):
    return lax.dot_general(lhs, rhs, (((1,), (0,)), ((), ())), preferred_element_type=F32)


def _pieces(n_vir, moved):
    spare = LANES - n_vir
    slots = []
    for t in range(-(-moved * n_vir // spare)):
        runs = []
        col, end = t * spare, min((t + 1) * spare, moved * n_vir)
        at = n_vir
        while col < end:
            count = min(end, (col // n_vir + 1) * n_vir) - col
            runs.append((col // n_vir, col % n_vir, at, count))
            col, at = col + count, at + count
        slots.append(runs)
    return slots


def _kernel(n_dev, rows, n_ao, n_occ, n_vir, q_chunk, n_buf, pitch, keep,
            a_hbm, cot_ref, cv_ref, v1_ref, v2_ref,
            abuf, tb0, tb1, w2, ct, sb, rb, rep, wk, acc1, acc2, asem, ssem, rsem):
    me = lax.axis_index('dev')
    n_chunk = n_ao // q_chunk
    total = rows * n_chunk
    moved = (n_occ + n_vir) // GROUP - keep
    slots = _pieces(n_vir, moved)
    block_rows = keep * GROUP

    def fetch(chunk):
        slot = lax.rem(chunk, n_buf)
        return pltpu.make_async_copy(
            a_hbm.at[chunk // n_chunk, pl.ds(lax.rem(chunk, n_chunk) * q_chunk, q_chunk)],
            abuf.at[slot], asem.at[slot])

    for first in range(n_buf):
        fetch(jnp.int32(first)).start()

    barrier = pltpu.get_barrier_semaphore()

    @pl.loop(1, n_dev)
    def _(k):
        pl.semaphore_signal(barrier, inc=1, device_id={'dev': lax.rem(me + k, n_dev)},
                            device_id_type=pl.DeviceIdType.MESH)

    w2[...] = jnp.zeros_like(w2)
    w2[:n_ao, :n_vir] = cv_ref[...]
    w2[:n_ao, LANES:LANES + n_occ] = cot_ref[...].astype(F32).T.astype(BF16)
    ct[:n_occ, :] = cot_ref[...]
    ct[n_occ:, :] = cv_ref[...].astype(F32).T.astype(BF16)
    acc1[...] = jnp.zeros_like(acc1)
    acc2[...] = jnp.zeros_like(acc2)
    lane = lax.broadcasted_iota(jnp.int32, (GROUP, LANES), 1)

    pl.semaphore_wait(barrier, n_dev - 1)

    def send(row, x):
        return pltpu.make_async_remote_copy(
            src_ref=sb.at[row, x], dst_ref=rb.at[row, me],
            send_sem=ssem.at[row], recv_sem=rsem.at[row],
            device_id={'dev': x}, device_id_type=pl.DeviceIdType.MESH)

    @pl.loop(0, rows)
    def _(row):
        @pl.loop(0, n_chunk)
        def _(part):
            chunk = row * n_chunk + part
            slot = lax.rem(chunk, n_buf)
            fetch(chunk).wait()

            @pl.loop(0, q_chunk // 8)
            def _(block):
                for u in range(8):
                    q = block * 8 + u
                    t = _dot(cot_ref[...], abuf[slot, q])
                    at = pl.ds(part * q_chunk + q, n_occ, stride=pitch)
                    tb0[at, :] = t[:, :LANES]
                    tb1[at, :] = jnp.pad(t[:, LANES:], ((0, 0), (0, 2 * LANES - n_ao)))

            @pl.when(chunk + n_buf < total)
            def _():
                fetch(chunk + n_buf).start()

        @pl.loop(0, n_dev)
        def _(step):
            x = lax.rem(me + 1 + step, n_dev)
            at = pl.ds(pl.multiple_of(x * pitch, 8), n_ao)
            t = jnp.concatenate([tb0[at, :].astype(BF16), tb1[at, :].astype(BF16)], axis=1)
            h = _dot(t, w2[...])
            hov = h[:, :LANES].astype(BF16)
            hoo = h[:, LANES:LANES + n_occ].T.astype(BF16)
            gov = _dot(ct[n_occ:, :], hov)
            goo = _dot(hoo, w2[:n_ao, :LANES])
            groups = [goo[g * GROUP:(g + 1) * GROUP] for g in range(n_occ // GROUP)]
            groups += [gov[g * GROUP:(g + 1) * GROUP] for g in range(n_vir // GROUP)]
            out = []
            for t_, value in enumerate(groups[:keep]):
                for group, src, dst, _count in (slots[t_] if t_ < len(slots) else ()):
                    tail = groups[keep + group]
                    if (dst - src) % LANES:
                        tail = pltpu.roll(tail, (dst - src) % LANES, 1)
                    value = jnp.where(lane < dst, value, tail)
                out.append(value)
            sb[row, x] = jnp.concatenate(out, axis=0).astype(BF16)

            @pl.when(step > 0)
            def _():
                send(row, lax.rem(me + step, n_dev)).start()

        rb[row, me] = sb[row, me]

    ident = (lax.broadcasted_iota(jnp.int32, (TILE, n_dev * TILE), 1) % TILE
             == lax.broadcasted_iota(jnp.int32, (TILE, n_dev * TILE), 0))
    owner = (lax.broadcasted_iota(jnp.int32, (n_ao, n_dev * TILE), 1) // TILE) * rows
    place = lax.broadcasted_iota(jnp.int32, (n_ao, n_dev * TILE), 0)
    n_tile = block_rows // TILE
    oo_rows = n_occ * TILE

    @pl.loop(0, rows)
    def _(row):
        pick = jnp.where(place == owner + row, 1.0, 0.0).astype(BF16)
        rep[...] = _dot(ct[...], pick)

        @pl.loop(0, (n_occ + n_vir) // 8)
        def _(block):
            for u in range(8):
                i = block * 8 + u
                value = jnp.where(ident, rep[pl.ds(i, 1), :], 0.0).astype(BF16)
                wk[pl.ds(pl.multiple_of(i * TILE, TILE), TILE), :] = value

        pltpu.make_async_copy(rb.at[row, pl.ds(0, n_dev - 1)], rb.at[row, pl.ds(0, n_dev - 1)],
                              rsem.at[row]).wait()

        def tiles(first, count):
            parts = [rb[row, :, t * TILE:(t + 1) * TILE, :].reshape(n_dev * TILE, LANES)
                     for t in range(first, first + count)]
            return parts[0] if count == 1 else jnp.concatenate(parts, axis=1)

        for first in range(0, n_tile, 2):
            count = min(2, n_tile - first)
            out = _dot(wk[:oo_rows, :], tiles(first, count))
            for c in range(count):
                at = slice((first + c) * TILE, (first + c + 1) * TILE)
                acc2[:, at, :] += out[:, c * LANES:(c + 1) * LANES].reshape(n_occ, TILE, LANES)

        n_block = n_vir // GROUP
        rhs = tiles(0, n_occ // TILE)

        @pl.loop(0, n_block)
        def _(block):
            at = pl.ds(pl.multiple_of(oo_rows + block * (GROUP * TILE), TILE), GROUP * TILE)
            out = _dot(wk[at, :], rhs)
            for c in range(n_occ // TILE):
                acc1[pl.ds(block * GROUP, GROUP), c * TILE:(c + 1) * TILE, :] += (
                    out[:, c * LANES:(c + 1) * LANES].reshape(GROUP, TILE, LANES))

    v1_ref[...] = acc1[:, :, :n_vir]
    head = n_vir // GROUP - moved
    v2_ref[:, :head * GROUP, :] = acc2[:, n_occ:n_occ + head * GROUP, :n_vir]

    @pl.loop(0, n_occ)
    def _(i):
        for group in range(moved):
            value = None
            for t, runs in enumerate(slots):
                for g, src, dst, _count in runs:
                    if g == group:
                        piece = acc2[i, t * GROUP:(t + 1) * GROUP, :]
                        if (src - dst) % LANES:
                            piece = pltpu.roll(piece, (src - dst) % LANES, 1)
                        value = piece if value is None else jnp.where(lane < src, value, piece)
            v2_ref[i, (head + group) * GROUP:(head + group + 1) * GROUP, :] = value[:, :n_vir]

    for row in range(rows):
        pltpu.make_async_copy(sb.at[row, pl.ds(0, n_dev - 1)], sb.at[row, pl.ds(0, n_dev - 1)],
                              ssem.at[row]).wait()


def solution(mesh):
    n_dev = mesh.shape['dev']

    def local_part(ao_rows, c_occ, c_vir):
        rows, n_ao = ao_rows.shape[:2]
        n_occ, n_vir = c_occ.shape[1], c_vir.shape[1]
        assert n_occ == n_dev
        q_chunk, n_buf, pitch = 32, 3, n_ao + 8
        keep = 14
        block_rows = keep * GROUP
        n_mo = n_occ + n_vir
        v1, v2 = pl.pallas_call(
            functools.partial(_kernel, n_dev, rows, n_ao, n_occ, n_vir, q_chunk, n_buf, pitch, keep),
            out_shape=(jax.ShapeDtypeStruct((n_vir, n_occ, n_vir), F32),
                       jax.ShapeDtypeStruct((n_occ, n_vir, n_vir), F32)),
            in_specs=[pl.BlockSpec(memory_space=pl.ANY),
                      pl.BlockSpec(memory_space=pltpu.VMEM),
                      pl.BlockSpec(memory_space=pltpu.VMEM)],
            out_specs=(pl.BlockSpec(memory_space=pltpu.VMEM), pl.BlockSpec(memory_space=pltpu.VMEM)),
            scratch_shapes=[
                pltpu.VMEM((n_buf, q_chunk, n_ao, n_ao), BF16),
                pltpu.VMEM((n_occ * pitch, LANES), F32),
                pltpu.VMEM((n_occ * pitch, LANES), F32),
                pltpu.VMEM((2 * LANES, 2 * LANES), BF16),
                pltpu.VMEM((n_mo, n_ao), BF16),
                pltpu.VMEM((rows, n_dev, block_rows, LANES), BF16),
                pltpu.VMEM((rows, n_dev, block_rows, LANES), BF16),
                pltpu.VMEM((n_mo, n_dev * TILE), F32),
                pltpu.VMEM((n_mo * TILE, n_dev * TILE), BF16),
                pltpu.VMEM((n_vir, n_occ, LANES), F32),
                pltpu.VMEM((n_occ, block_rows, LANES), F32),
                pltpu.SemaphoreType.DMA((n_buf,)),
                pltpu.SemaphoreType.DMA((rows,)),
                pltpu.SemaphoreType.DMA((rows,)),
            ],
            compiler_params=pltpu.CompilerParams(collective_id=0, has_side_effects=True,
                                                 vmem_limit_bytes=60 * 1024 * 1024),
        )(ao_rows, c_occ.T, c_vir)
        return v1.transpose(0, 2, 1), v2

    return jax.shard_map(local_part, mesh=mesh,
                         in_specs=(P(('frag', 'dev')), P('frag'), P('frag')),
                         out_specs=(P('frag', None, 'dev'), P('frag', None, 'dev')),
                         check_vma=False)
```

time: 267 us -> 132 us (0.49)
  the two profiles are of different devices: /device:TPU:103 before, /device:TPU:97 now
where the time goes in v1:
time: 132 us
  Pallas kernels  127 us (96%)
  local copies, waits for them, and re-layouts  4.09 us (3%)
    pallas_call x1, Pallas kernels, local_part(): pl.pallas_call(functools.partial(_kernel, n_dev, rows, n_ao, n_occ, n_vir...  127 us
    unnamed x4, local copies, waits for them, and re-layouts  4.09 us

profile of v1, /device:TPU:97, one launch (start us, length us, event | category | flops | bytes accessed | tf_op | source)
XLA Modules:
  0.0 131.6 jit_solution(7154959915209149798)
XLA Ops:
  0.6 126.9 %shard_map.50 = (f32[104,32,104]{2,1,0:T(8,128)}, f32[32,104,104]{2,1,0:T(8,128)}) custom-call(bf16[5,160,160,160]{3,2,1,0:T(8,128)(2,1)} %a_hbm.1, bf16[32,160]{1,0:T(8,128)(2,1)} %bitcast.3, bf16[160,104]{1,0:T(8,128)(2,1)} %cv_ref.1), custom_call_target="tpu_custom_call" | custom-call | tf_op jit(solution)/shard_map/pallas_call | solution.py:206
  127.5 0.0 copy-start
  127.5 2.9 %copy.7 = f32[104,104,32]{1,2,0:T(8,128)} copy(f32[104,104,32]{1,2,0:T(8,128)} %bitcast.2) | data formatting | bytes 2768896
  130.4 0.0 copy-done
  130.4 1.2 copy.8
Async XLA Ops:
  127.5 2.9 %copy-start = (f32[32,104,104]{2,1,0:T(8,128)S(1)}, f32[32,104,104]{2,1,0:T(8,128)}, u32[]{:S(2)}) copy-start(f32[32,104,104]{2,1,0:T(8,128)} %get-tuple-element.9) | copy-start | bytes 4153348

commit v2 on v1

--- a/solution.py
+++ b/solution.py
@@ -33,10 +33,11 @@
     return slots
 
 
-def _kernel(n_dev, rows, n_ao, n_occ, n_vir, q_chunk, n_buf, pitch, keep,
+def _kernel(n_dev, rows, n_ao, n_occ, n_vir, q_chunk, n_buf, pitch, keep, unroll,
             a_hbm, cot_ref, cv_ref, v1_ref, v2_ref,
-            abuf, tb0, tb1, w2, ct, sb, rb, rep, wk, acc1, acc2, asem, ssem, rsem):
+            abuf, tb0, tb1, w2, ct, hov0, hov1, hoo0, hoo1, sb, rb, rep, wk, acc1, acc2, asem, ssem, rsem):
     me = lax.axis_index('dev')
+    hov, hoo = (hov0, hov1), (hoo0, hoo1)
     n_chunk = n_ao // q_chunk
     total = rows * n_chunk
     moved = (n_occ + n_vir) // GROUP - keep
@@ -84,46 +85,61 @@
             slot = lax.rem(chunk, n_buf)
             fetch(chunk).wait()
 
-            @pl.loop(0, q_chunk // 8)
-            def _(block):
-                for u in range(8):
-                    q = block * 8 + u
-                    t = _dot(cot_ref[...], abuf[slot, q])
-                    at = pl.ds(part * q_chunk + q, n_occ, stride=pitch)
-                    tb0[at, :] = t[:, :LANES]
-                    tb1[at, :] = jnp.pad(t[:, LANES:], ((0, 0), (0, 2 * LANES - n_ao)))
+            for q in range(q_chunk):
+                t = _dot(cot_ref[...], abuf[slot, q])
+                at = pl.ds(part * q_chunk + q, n_occ, stride=pitch)
+                tb0[at, :] = t[:, :LANES]
+                tb1[at, :] = jnp.pad(t[:, LANES:], ((0, 0), (0, 2 * LANES - n_ao)))
 
             @pl.when(chunk + n_buf < total)
             def _():
                 fetch(chunk + n_buf).start()
 
-        @pl.loop(0, n_dev)
-        def _(step):
-            x = lax.rem(me + 1 + step, n_dev)
-            at = pl.ds(pl.multiple_of(x * pitch, 8), n_ao)
-            t = jnp.concatenate([tb0[at, :].astype(BF16), tb1[at, :].astype(BF16)], axis=1)
-            h = _dot(t, w2[...])
-            hov = h[:, :LANES].astype(BF16)
-            hoo = h[:, LANES:LANES + n_occ].T.astype(BF16)
-            gov = _dot(ct[n_occ:, :], hov)
-            goo = _dot(hoo, w2[:n_ao, :LANES])
-            groups = [goo[g * GROUP:(g + 1) * GROUP] for g in range(n_occ // GROUP)]
-            groups += [gov[g * GROUP:(g + 1) * GROUP] for g in range(n_vir // GROUP)]
-            out = []
-            for t_, value in enumerate(groups[:keep]):
-                for group, src, dst, _count in (slots[t_] if t_ < len(slots) else ()):
-                    tail = groups[keep + group]
-                    if (dst - src) % LANES:
-                        tail = pltpu.roll(tail, (dst - src) % LANES, 1)
-                    value = jnp.where(lane < dst, value, tail)
-                out.append(value)
-            sb[row, x] = jnp.concatenate(out, axis=0).astype(BF16)
-
-            @pl.when(step > 0)
-            def _():
-                send(row, lax.rem(me + step, n_dev)).start()
-
+        def owner_of(step):
+            return lax.rem(me + 1 + step, n_dev)
+
+        def half(group):
+            parts = []
+            for u in range(unroll):
+                at = pl.ds(pl.multiple_of(owner_of(group * unroll + u) * pitch, 8), n_ao)
+                parts.append(jnp.concatenate([tb0[at, :].astype(BF16), tb1[at, :].astype(BF16)], axis=1))
+            h = _dot(jnp.concatenate(parts, axis=0), w2[...])
+            for u in range(unroll):
+                at = slice(u * n_ao, (u + 1) * n_ao)
+                hov[group % 2][u] = h[at, :LANES].astype(BF16)
+                hoo[group % 2][u * n_occ:(u + 1) * n_occ, :] = h[at, LANES:LANES + n_occ].T.astype(BF16)
+
+        def full(group):
+            goo = _dot(hoo[group % 2][...], w2[:n_ao, :LANES])
+            for u in range(0, unroll, 2):
+                pair = _dot(ct[n_occ:, :], jnp.concatenate([hov[group % 2][u], hov[group % 2][u + 1]], axis=1))
+                for v in range(2):
+                    gov = pair[:, v * LANES:(v + 1) * LANES]
+                    first = (u + v) * n_occ
+                    groups = [goo[first + g * GROUP:first + (g + 1) * GROUP] for g in range(n_occ // GROUP)]
+                    groups += [gov[g * GROUP:(g + 1) * GROUP] for g in range(n_vir // GROUP)]
+                    out = []
+                    for t_, value in enumerate(groups[:keep]):
+                        for part, src, dst, _count in (slots[t_] if t_ < len(slots) else ()):
+                            tail = groups[keep + part]
+                            if (dst - src) % LANES:
+                                tail = pltpu.roll(tail, (dst - src) % LANES, 1)
+                            value = jnp.where(lane < dst, value, tail)
+                        out.append(value)
+                    sb[row, owner_of(group * unroll + u + v)] = jnp.concatenate(out, axis=0).astype(BF16)
+
+        n_group = n_dev // unroll
+        half(0)
+        for group in range(n_group):
+            if group + 1 < n_group:
+                half(group + 1)
+            full(group)
+            if group:
+                for u in range(unroll):
+                    send(row, owner_of((group - 1) * unroll + u)).start()
         rb[row, me] = sb[row, me]
+        for u in range(unroll - 1):
+            send(row, owner_of((n_group - 1) * unroll + u)).start()
 
     ident = (lax.broadcasted_iota(jnp.int32, (TILE, n_dev * TILE), 1) % TILE
              == lax.broadcasted_iota(jnp.int32, (TILE, n_dev * TILE), 0))
@@ -159,16 +175,17 @@
                 at = slice((first + c) * TILE, (first + c + 1) * TILE)
                 acc2[:, at, :] += out[:, c * LANES:(c + 1) * LANES].reshape(n_occ, TILE, LANES)
 
-        n_block = n_vir // GROUP
+        n_block = 4
+        span = n_vir // n_block
         rhs = tiles(0, n_occ // TILE)
 
         @pl.loop(0, n_block)
         def _(block):
-            at = pl.ds(pl.multiple_of(oo_rows + block * (GROUP * TILE), TILE), GROUP * TILE)
+            at = pl.ds(pl.multiple_of(oo_rows + block * (span * TILE), TILE), span * TILE)
             out = _dot(wk[at, :], rhs)
             for c in range(n_occ // TILE):
-                acc1[pl.ds(block * GROUP, GROUP), c * TILE:(c + 1) * TILE, :] += (
-                    out[:, c * LANES:(c + 1) * LANES].reshape(GROUP, TILE, LANES))
+                acc1[pl.ds(block * span, span), c * TILE:(c + 1) * TILE, :] += (
+                    out[:, c * LANES:(c + 1) * LANES].reshape(span, TILE, LANES))
 
     v1_ref[...] = acc1[:, :, :n_vir]
     head = n_vir // GROUP - moved
@@ -200,11 +217,11 @@
         n_occ, n_vir = c_occ.shape[1], c_vir.shape[1]
         assert n_occ == n_dev
         q_chunk, n_buf, pitch = 32, 3, n_ao + 8
-        keep = 14
+        keep, unroll = 14, 8
         block_rows = keep * GROUP
         n_mo = n_occ + n_vir
         v1, v2 = pl.pallas_call(
-            functools.partial(_kernel, n_dev, rows, n_ao, n_occ, n_vir, q_chunk, n_buf, pitch, keep),
+            functools.partial(_kernel, n_dev, rows, n_ao, n_occ, n_vir, q_chunk, n_buf, pitch, keep, unroll),
             out_shape=(jax.ShapeDtypeStruct((n_vir, n_occ, n_vir), F32),
                        jax.ShapeDtypeStruct((n_occ, n_vir, n_vir), F32)),
             in_specs=[pl.BlockSpec(memory_space=pl.ANY),
@@ -217,6 +234,10 @@
                 pltpu.VMEM((n_occ * pitch, LANES), F32),
                 pltpu.VMEM((2 * LANES, 2 * LANES), BF16),
                 pltpu.VMEM((n_mo, n_ao), BF16),
+                pltpu.VMEM((unroll, n_ao, LANES), BF16),
+                pltpu.VMEM((unroll, n_ao, LANES), BF16),
+                pltpu.VMEM((unroll * n_occ, n_ao), BF16),
+                pltpu.VMEM((unroll * n_occ, n_ao), BF16),
                 pltpu.VMEM((rows, n_dev, block_rows, LANES), BF16),
                 pltpu.VMEM((rows, n_dev, block_rows, LANES), BF16),
                 pltpu.VMEM((n_mo, n_dev * TILE), F32),

time: 132 us -> 81.7 us (0.62)
  the two profiles are of different devices: /device:TPU:97 before, /device:TPU:103 now
where the time goes in v2:
time: 81.7 us; the launch traced here: 81.5 us
  Pallas kernels  76.8 us (94%)
  local copies, waits for them, and re-layouts  4.09 us (5%)
    pallas_call x1, Pallas kernels, local_part(): pl.pallas_call(functools.partial(_kernel, n_dev, rows, n_ao, n_occ, n_vir...  76.8 us
    unnamed x4, local copies, waits for them, and re-layouts  4.09 us

profile of v2, /device:TPU:103, one launch (start us, length us, event | category | flops | bytes accessed | tf_op | source)
XLA Modules:
  0.0 81.5 jit_solution(1132644315310589706)
XLA Ops:
  0.6 76.8 %shard_map.50 = (f32[104,32,104]{2,1,0:T(8,128)}, f32[32,104,104]{2,1,0:T(8,128)}) custom-call(bf16[5,160,160,160]{3,2,1,0:T(8,128)(2,1)} %a_hbm.1, bf16[32,160]{1,0:T(8,128)(2,1)} %bitcast.3, bf16[160,104]{1,0:T(8,128)(2,1)} %cv_ref.1), custom_call_target="tpu_custom_call" | custom-call | tf_op jit(solution)/shard_map/pallas_call | solution.py:223
  77.4 0.0 copy-start
  77.4 2.9 %copy.7 = f32[104,104,32]{1,2,0:T(8,128)} copy(f32[104,104,32]{1,2,0:T(8,128)} %bitcast.2) | data formatting | bytes 2768896
  80.3 0.0 copy-done
  80.3 1.2 %copy.8 = f32[32,104,104]{2,1,0:T(8,128)} copy(f32[32,104,104]{2,1,0:T(8,128)S(1)} %copy-done) | data formatting | bytes 2768896
Async XLA Ops:
  77.4 2.9 %copy-start = (f32[32,104,104]{2,1,0:T(8,128)S(1)}, f32[32,104,104]{2,1,0:T(8,128)}, u32[]{:S(2)}) copy-start(f32[32,104,104]{2,1,0:T(8,128)} %get-tuple-element.9) | copy-start | bytes 4153348

commit v3 on v2

--- a/solution.py
+++ b/solution.py
@@ -1,4 +1,5 @@
 import functools
+import math
 
 import jax
 import jax.numpy as jnp
@@ -33,11 +34,30 @@
     return slots
 
 
+def _order(side):
+    def hops(d):
+        return min(d, side - d)
+
+    left = {(dx, dy) for dx in range(side) for dy in range(side)}
+    chips = []
+    for dx, dy in sorted(left, key=lambda c: (-(hops(c[0]) > 0) - (hops(c[1]) > 0),
+                                              abs(hops(c[0]) - hops(c[1])), hops(c[0]), c)):
+        for chip in ((dx, dy), (-dx % side, -dy % side), (dy, -dx % side), (-dy % side, dx)):
+            if chip in left:
+                left.remove(chip)
+                chips.append(chip)
+    return [(dx, dy, other) for dx, dy in chips for other in (1, 0)]
+
+
 def _kernel(n_dev, rows, n_ao, n_occ, n_vir, q_chunk, n_buf, pitch, keep, unroll,
-            a_hbm, cot_ref, cv_ref, v1_ref, v2_ref,
-            abuf, tb0, tb1, w2, ct, hov0, hov1, hoo0, hoo1, sb, rb, rep, wk, acc1, acc2, asem, ssem, rsem):
+            a_hbm, cot_ref, cv_ref, acc1, acc2,
+            abuf, tb0, tb1, w2, ct, hov0, hov1, hoo0, hoo1, sb, rb, rep, wk, asem, ssem, rsem):
     me = lax.axis_index('dev')
     hov, hoo = (hov0, hov1), (hoo0, hoo1)
+    side = math.isqrt(n_dev // 2)
+    core, cx, cy = lax.rem(me, 2), lax.rem(me // 2, side), me // (2 * side)
+    sign = 1 - 2 * core
+    order = _order(side)
     n_chunk = n_ao // q_chunk
     total = rows * n_chunk
     moved = (n_occ + n_vir) // GROUP - keep
@@ -96,7 +116,9 @@
                 fetch(chunk + n_buf).start()
 
         def owner_of(step):
-            return lax.rem(me + 1 + step, n_dev)
+            dx, dy, other = order[step]
+            return ((lax.rem(cy + dy * sign + side, side) * side + lax.rem(cx + dx * sign + side, side)) * 2
+                    + lax.rem(core + other, 2))
 
         def half(group):
             parts = []
@@ -185,28 +207,41 @@
             out = _dot(wk[at, :], rhs)
             for c in range(n_occ // TILE):
                 acc1[pl.ds(block * span, span), c * TILE:(c + 1) * TILE, :] += (
-                    out[:, c * LANES:(c + 1) * LANES].reshape(span, TILE, LANES))
-
-    v1_ref[...] = acc1[:, :, :n_vir]
-    head = n_vir // GROUP - moved
-    v2_ref[:, :head * GROUP, :] = acc2[:, n_occ:n_occ + head * GROUP, :n_vir]
-
-    @pl.loop(0, n_occ)
-    def _(i):
-        for group in range(moved):
-            value = None
-            for t, runs in enumerate(slots):
-                for g, src, dst, _count in runs:
-                    if g == group:
-                        piece = acc2[i, t * GROUP:(t + 1) * GROUP, :]
-                        if (src - dst) % LANES:
-                            piece = pltpu.roll(piece, (src - dst) % LANES, 1)
-                        value = piece if value is None else jnp.where(lane < src, value, piece)
-            v2_ref[i, (head + group) * GROUP:(head + group + 1) * GROUP, :] = value[:, :n_vir]
+                    out[:, c * LANES:c * LANES + n_vir].reshape(span, TILE, n_vir))
 
     for row in range(rows):
         pltpu.make_async_copy(sb.at[row, pl.ds(0, n_dev - 1)], sb.at[row, pl.ds(0, n_dev - 1)],
                               ssem.at[row]).wait()
+
+
+def _unpack(n_occ, n_vir, keep, acc1, acc2, v1_ref, v2_ref, v2, sem):
+    moved = (n_occ + n_vir) // GROUP - keep
+    head = n_vir // GROUP - moved
+    slots = _pieces(n_vir, moved)
+    lane = lax.broadcasted_iota(jnp.int32, (GROUP, LANES), 1)
+    first = pltpu.make_async_copy(acc1, v1_ref, sem.at[0])
+    first.start()
+
+    @pl.loop(0, n_occ // 4)
+    def _(block):
+        for u in range(4):
+            i = block * 4 + u
+            v2[i, :head * GROUP, :] = acc2[i, n_occ:n_occ + head * GROUP, :n_vir]
+            for group in range(moved):
+                value = None
+                for t, runs in enumerate(slots):
+                    for g, src, dst, _count in runs:
+                        if g == group:
+                            piece = acc2[i, t * GROUP:(t + 1) * GROUP, :]
+                            if (src - dst) % LANES:
+                                piece = pltpu.roll(piece, (src - dst) % LANES, 1)
+                            value = piece if value is None else jnp.where(lane < src, value, piece)
+                v2[i, (head + group) * GROUP:(head + group + 1) * GROUP, :] = value[:, :n_vir]
+
+    second = pltpu.make_async_copy(v2, v2_ref, sem.at[1])
+    second.start()
+    first.wait()
+    second.wait()
 
 
 def solution(mesh):
@@ -220,10 +255,10 @@
         keep, unroll = 14, 8
         block_rows = keep * GROUP
         n_mo = n_occ + n_vir
-        v1, v2 = pl.pallas_call(
+        acc1, acc2 = pl.pallas_call(
             functools.partial(_kernel, n_dev, rows, n_ao, n_occ, n_vir, q_chunk, n_buf, pitch, keep, unroll),
-            out_shape=(jax.ShapeDtypeStruct((n_vir, n_occ, n_vir), F32),
-                       jax.ShapeDtypeStruct((n_occ, n_vir, n_vir), F32)),
+            out_shape=(pltpu.VMEM((n_vir, n_occ, n_vir), F32),
+                       pltpu.VMEM((n_occ, block_rows, LANES), F32)),
             in_specs=[pl.BlockSpec(memory_space=pl.ANY),
                       pl.BlockSpec(memory_space=pltpu.VMEM),
                       pl.BlockSpec(memory_space=pltpu.VMEM)],
@@ -242,15 +277,22 @@
                 pltpu.VMEM((rows, n_dev, block_rows, LANES), BF16),
                 pltpu.VMEM((n_mo, n_dev * TILE), F32),
                 pltpu.VMEM((n_mo * TILE, n_dev * TILE), BF16),
-                pltpu.VMEM((n_vir, n_occ, LANES), F32),
-                pltpu.VMEM((n_occ, block_rows, LANES), F32),
                 pltpu.SemaphoreType.DMA((n_buf,)),
                 pltpu.SemaphoreType.DMA((rows,)),
                 pltpu.SemaphoreType.DMA((rows,)),
             ],
             compiler_params=pltpu.CompilerParams(collective_id=0, has_side_effects=True,
-                                                 vmem_limit_bytes=60 * 1024 * 1024),
+                                                 vmem_limit_bytes=44 * 1024 * 1024),
         )(ao_rows, c_occ.T, c_vir)
+        v1, v2 = pl.pallas_call(
+            functools.partial(_unpack, n_occ, n_vir, keep),
+            out_shape=(jax.ShapeDtypeStruct((n_vir, n_occ, n_vir), F32),
+                       jax.ShapeDtypeStruct((n_occ, n_vir, n_vir), F32)),
+            in_specs=[pl.BlockSpec(memory_space=pltpu.VMEM)] * 2,
+            out_specs=(pl.BlockSpec(memory_space=pl.ANY), pl.BlockSpec(memory_space=pl.ANY)),
+            scratch_shapes=[pltpu.VMEM((n_occ, n_vir, n_vir), F32), pltpu.SemaphoreType.DMA((2,))],
+            compiler_params=pltpu.CompilerParams(vmem_limit_bytes=8 * 1024 * 1024),
+        )(acc1, acc2)
         return v1.transpose(0, 2, 1), v2
 
     return jax.shard_map(local_part, mesh=mesh,

time: 81.7 us -> 75 us (0.918)
  the two profiles are of different devices: /device:TPU:103 before, /device:TPU:97 now
where the time goes in v3:
time: 75 us; the launch traced here: 74.7 us
  Pallas kernels  72.6 us (97%)
  local copies, waits for them, and re-layouts  1.49 us (2%)
    pallas_call x1, Pallas kernels, local_part(): pl.pallas_call(functools.partial(_kernel, n_dev, rows, n_ao, n_occ, n_vir...  70.3 us
    pallas_call x1, Pallas kernels, local_part(): pl.pallas_call(functools.partial(_unpack, n_occ, n_vir, keep), out_shape=...  2.27 us

profile of v3, /device:TPU:97, one launch (start us, length us, event | category | flops | bytes accessed | tf_op | source)
XLA Modules:
  0.0 74.7 jit_solution(14505645681537737597)
XLA Ops:
  0.6 0.0 copy-start
  0.6 0.8 %copy-done = bf16[160,104]{1,0:T(8,128)(2,1)S(1)} copy-done((bf16[160,104]{1,0:T(8,128)(2,1)S(1)}, bf16[160,104]{1,0:T(8,128)(2,1)}, u32[]{:S(2)}) %copy-start) | copy-done | bytes 33304
  1.4 0.0 copy-start.1
  1.4 0.7 copy-done.1
  2.1 70.3 %shard_map.50 = (f32[104,32,104]{2,1,0:T(8,128)S(1)}, f32[32,112,128]{2,1,0:T(8,128)S(1)}) custom-call(bf16[5,160,160,160]{3,2,1,0:T(8,128)(2,1)} %a_hbm.1, bf16[32,160]{1,0:T(8,128)(2,1)S(1)} %bitcast.2, bf16[160,104]{1,0:T(8,128)(2,1)S(1)} %copy-done), custom_call_target="tpu_custom_call" | custom-call | tf_op jit(solution)/shard_map/pallas_call | solution.py:258
  72.5 2.3 %shard_map.51 = (f32[104,32,104]{2,1,0:T(8,128)}, f32[32,104,104]{2,1,0:T(8,128)}) custom-call(f32[104,32,104]{2,1,0:T(8,128)S(1)} %get-tuple-element.6.acc1, f32[32,112,128]{2,1,0:T(8,128)S(1)} %get-tuple-element.7.acc2), custom_call_target="tpu_custom_call" | custom-call | tf_op jit(solution)/shard_map/pallas_call | solution.py:287
Async XLA Ops:
  0.6 0.8 %copy-start = (bf16[160,104]{1,0:T(8,128)(2,1)S(1)}, bf16[160,104]{1,0:T(8,128)(2,1)}, u32[]{:S(2)}) copy-start(bf16[160,104]{1,0:T(8,128)(2,1)} %cv_ref.1) | copy-start | bytes 99844
  1.4 0.7 copy-start.1

commit v4 on v2

--- a/solution.py
+++ b/solution.py
@@ -34,11 +34,12 @@
 
 
 def _kernel(n_dev, rows, n_ao, n_occ, n_vir, q_chunk, n_buf, pitch, keep, unroll,
-            a_hbm, cot_ref, cv_ref, v1_ref, v2_ref,
-            abuf, tb0, tb1, w2, ct, hov0, hov1, hoo0, hoo1, sb, rb, rep, wk, acc1, acc2, asem, ssem, rsem):
+            a_hbm, cot_hbm, cv_hbm, acc1, acc2,
+            cot_ref, cv_ref, abuf, tb0, tb1, w2, ct, hov0, hov1, hoo0, hoo1, sb, rb, rep, wk, csem, asem, ssem, rsem):
     me = lax.axis_index('dev')
     hov, hoo = (hov0, hov1), (hoo0, hoo1)
     n_chunk = n_ao // q_chunk
+    n_half = n_dev // 2
     total = rows * n_chunk
     moved = (n_occ + n_vir) // GROUP - keep
     slots = _pieces(n_vir, moved)
@@ -50,6 +51,10 @@
             a_hbm.at[chunk // n_chunk, pl.ds(lax.rem(chunk, n_chunk) * q_chunk, q_chunk)],
             abuf.at[slot], asem.at[slot])
 
+    coefs = (pltpu.make_async_copy(cot_hbm, cot_ref, csem.at[0]),
+             pltpu.make_async_copy(cv_hbm, cv_ref, csem.at[1]))
+    for copy in coefs:
+        copy.start()
     for first in range(n_buf):
         fetch(jnp.int32(first)).start()
 
@@ -60,22 +65,25 @@
         pl.semaphore_signal(barrier, inc=1, device_id={'dev': lax.rem(me + k, n_dev)},
                             device_id_type=pl.DeviceIdType.MESH)
 
+    acc1[...] = jnp.zeros_like(acc1)
+    acc2[...] = jnp.zeros_like(acc2)
     w2[...] = jnp.zeros_like(w2)
+    for copy in coefs:
+        copy.wait()
+
     w2[:n_ao, :n_vir] = cv_ref[...]
     w2[:n_ao, LANES:LANES + n_occ] = cot_ref[...].astype(F32).T.astype(BF16)
     ct[:n_occ, :] = cot_ref[...]
     ct[n_occ:, :] = cv_ref[...].astype(F32).T.astype(BF16)
-    acc1[...] = jnp.zeros_like(acc1)
-    acc2[...] = jnp.zeros_like(acc2)
     lane = lax.broadcasted_iota(jnp.int32, (GROUP, LANES), 1)
 
     pl.semaphore_wait(barrier, n_dev - 1)
 
-    def send(row, x):
+    def send(row, step):
         return pltpu.make_async_remote_copy(
-            src_ref=sb.at[row, x], dst_ref=rb.at[row, me],
-            send_sem=ssem.at[row], recv_sem=rsem.at[row],
-            device_id={'dev': x}, device_id_type=pl.DeviceIdType.MESH)
+            src_ref=sb.at[row, step], dst_ref=rb.at[row, step],
+            send_sem=ssem.at[row], recv_sem=rsem.at[row, step // n_half],
+            device_id={'dev': lax.rem(me + 1 + step, n_dev)}, device_id_type=pl.DeviceIdType.MESH)
 
     @pl.loop(0, rows)
     def _(row):
@@ -126,7 +134,7 @@
                                 tail = pltpu.roll(tail, (dst - src) % LANES, 1)
                             value = jnp.where(lane < dst, value, tail)
                         out.append(value)
-                    sb[row, owner_of(group * unroll + u + v)] = jnp.concatenate(out, axis=0).astype(BF16)
+                    sb[row, group * unroll + u + v] = jnp.concatenate(out, axis=0).astype(BF16)
 
         n_group = n_dev // unroll
         half(0)
@@ -134,22 +142,21 @@
             if group + 1 < n_group:
                 half(group + 1)
             full(group)
-            if group:
-                for u in range(unroll):
-                    send(row, owner_of((group - 1) * unroll + u)).start()
-        rb[row, me] = sb[row, me]
-        for u in range(unroll - 1):
-            send(row, owner_of((n_group - 1) * unroll + u)).start()
+            first, last = group * unroll, (group + 1) * unroll
+            for step in range(max(first - 2, 0), last - 2):
+                send(row, step).start()
+        rb[row, n_dev - 1] = sb[row, n_dev - 1]
+        send(row, n_dev - 2).start()
 
     ident = (lax.broadcasted_iota(jnp.int32, (TILE, n_dev * TILE), 1) % TILE
              == lax.broadcasted_iota(jnp.int32, (TILE, n_dev * TILE), 0))
-    owner = (lax.broadcasted_iota(jnp.int32, (n_ao, n_dev * TILE), 1) // TILE) * rows
+    source = me - 1 - lax.broadcasted_iota(jnp.int32, (n_ao, n_dev * TILE), 1) // TILE
+    owner = jnp.where(source < 0, source + n_dev, source) * rows
     place = lax.broadcasted_iota(jnp.int32, (n_ao, n_dev * TILE), 0)
     n_tile = block_rows // TILE
     oo_rows = n_occ * TILE
 
-    @pl.loop(0, rows)
-    def _(row):
+    def weights(row):
         pick = jnp.where(place == owner + row, 1.0, 0.0).astype(BF16)
         rep[...] = _dot(ct[...], pick)
 
@@ -160,17 +167,21 @@
                 value = jnp.where(ident, rep[pl.ds(i, 1), :], 0.0).astype(BF16)
                 wk[pl.ds(pl.multiple_of(i * TILE, TILE), TILE), :] = value
 
-        pltpu.make_async_copy(rb.at[row, pl.ds(0, n_dev - 1)], rb.at[row, pl.ds(0, n_dev - 1)],
-                              rsem.at[row]).wait()
+    def arrived(row, part):
+        blocks = rb.at[row, pl.ds(part * n_half, n_half - part)]
+        pltpu.make_async_copy(blocks, blocks, rsem.at[row, part]).wait()
+
+    def contract(row, low, high):
+        cols = slice(low * TILE, high * TILE)
 
         def tiles(first, count):
-            parts = [rb[row, :, t * TILE:(t + 1) * TILE, :].reshape(n_dev * TILE, LANES)
+            parts = [rb[row, low:high, t * TILE:(t + 1) * TILE, :].reshape((high - low) * TILE, LANES)
                      for t in range(first, first + count)]
             return parts[0] if count == 1 else jnp.concatenate(parts, axis=1)
 
         for first in range(0, n_tile, 2):
             count = min(2, n_tile - first)
-            out = _dot(wk[:oo_rows, :], tiles(first, count))
+            out = _dot(wk[:oo_rows, cols], tiles(first, count))
             for c in range(count):
                 at = slice((first + c) * TILE, (first + c + 1) * TILE)
                 acc2[:, at, :] += out[:, c * LANES:(c + 1) * LANES].reshape(n_occ, TILE, LANES)
@@ -182,17 +193,37 @@
         @pl.loop(0, n_block)
         def _(block):
             at = pl.ds(pl.multiple_of(oo_rows + block * (span * TILE), TILE), span * TILE)
-            out = _dot(wk[at, :], rhs)
+            out = _dot(wk[at, cols], rhs)
             for c in range(n_occ // TILE):
                 acc1[pl.ds(block * span, span), c * TILE:(c + 1) * TILE, :] += (
-                    out[:, c * LANES:(c + 1) * LANES].reshape(span, TILE, LANES))
-
-    v1_ref[...] = acc1[:, :, :n_vir]
+                    out[:, c * LANES:c * LANES + n_vir].reshape(span, TILE, n_vir))
+
+    @pl.loop(0, rows - 1)
+    def _(row):
+        weights(row)
+        arrived(row, 0)
+        arrived(row, 1)
+        contract(row, 0, n_dev)
+
+    weights(rows - 1)
+    for part in range(2):
+        arrived(rows - 1, part)
+        contract(rows - 1, part * n_half, (part + 1) * n_half)
+
+    for row in range(rows):
+        pltpu.make_async_copy(sb.at[row, pl.ds(0, n_dev - 1)], sb.at[row, pl.ds(0, n_dev - 1)],
+                              ssem.at[row]).wait()
+
+
+def _unpack(n_occ, n_vir, keep, acc1, acc2, v1_ref, v2_ref, v2, sem):
+    moved = (n_occ + n_vir) // GROUP - keep
     head = n_vir // GROUP - moved
-    v2_ref[:, :head * GROUP, :] = acc2[:, n_occ:n_occ + head * GROUP, :n_vir]
-
-    @pl.loop(0, n_occ)
-    def _(i):
+    slots = _pieces(n_vir, moved)
+    lane = lax.broadcasted_iota(jnp.int32, (GROUP, LANES), 1)
+    copies = [pltpu.make_async_copy(acc1, v1_ref, sem.at[0])]
+    copies[0].start()
+    for i in range(n_occ):
+        v2[i, :head * GROUP, :] = acc2[i, n_occ:n_occ + head * GROUP, :n_vir]
         for group in range(moved):
             value = None
             for t, runs in enumerate(slots):
@@ -202,11 +233,13 @@
                         if (src - dst) % LANES:
                             piece = pltpu.roll(piece, (src - dst) % LANES, 1)
                         value = piece if value is None else jnp.where(lane < src, value, piece)
-            v2_ref[i, (head + group) * GROUP:(head + group + 1) * GROUP, :] = value[:, :n_vir]
-
-    for row in range(rows):
-        pltpu.make_async_copy(sb.at[row, pl.ds(0, n_dev - 1)], sb.at[row, pl.ds(0, n_dev - 1)],
-                              ssem.at[row]).wait()
+            v2[i, (head + group) * GROUP:(head + group + 1) * GROUP, :] = value[:, :n_vir]
+        if i % 8 == 7:
+            at = pl.ds(i - 7, 8)
+            copies.append(pltpu.make_async_copy(v2.at[at], v2_ref.at[at], sem.at[1 + i // 8]))
+            copies[-1].start()
+    for copy in copies:
+        copy.wait()
 
 
 def solution(mesh):
@@ -216,19 +249,19 @@
         rows, n_ao = ao_rows.shape[:2]
         n_occ, n_vir = c_occ.shape[1], c_vir.shape[1]
         assert n_occ == n_dev
-        q_chunk, n_buf, pitch = 32, 3, n_ao + 8
+        q_chunk, n_buf, pitch = 32, 5, n_ao + 8
         keep, unroll = 14, 8
         block_rows = keep * GROUP
         n_mo = n_occ + n_vir
-        v1, v2 = pl.pallas_call(
+        acc1, acc2 = pl.pallas_call(
             functools.partial(_kernel, n_dev, rows, n_ao, n_occ, n_vir, q_chunk, n_buf, pitch, keep, unroll),
-            out_shape=(jax.ShapeDtypeStruct((n_vir, n_occ, n_vir), F32),
-                       jax.ShapeDtypeStruct((n_occ, n_vir, n_vir), F32)),
-            in_specs=[pl.BlockSpec(memory_space=pl.ANY),
-                      pl.BlockSpec(memory_space=pltpu.VMEM),
-                      pl.BlockSpec(memory_space=pltpu.VMEM)],
+            out_shape=(pltpu.VMEM((n_vir, n_occ, n_vir), F32),
+                       pltpu.VMEM((n_occ, block_rows, LANES), F32)),
+            in_specs=[pl.BlockSpec(memory_space=pltpu.HBM)] * 3,
             out_specs=(pl.BlockSpec(memory_space=pltpu.VMEM), pl.BlockSpec(memory_space=pltpu.VMEM)),
             scratch_shapes=[
+                pltpu.VMEM((n_occ, n_ao), BF16),
+                pltpu.VMEM((n_ao, n_vir), BF16),
                 pltpu.VMEM((n_buf, q_chunk, n_ao, n_ao), BF16),
                 pltpu.VMEM((n_occ * pitch, LANES), F32),
                 pltpu.VMEM((n_occ * pitch, LANES), F32),
@@ -242,15 +275,23 @@
                 pltpu.VMEM((rows, n_dev, block_rows, LANES), BF16),
                 pltpu.VMEM((n_mo, n_dev * TILE), F32),
                 pltpu.VMEM((n_mo * TILE, n_dev * TILE), BF16),
-                pltpu.VMEM((n_vir, n_occ, LANES), F32),
-                pltpu.VMEM((n_occ, block_rows, LANES), F32),
+                pltpu.SemaphoreType.DMA((2,)),
                 pltpu.SemaphoreType.DMA((n_buf,)),
                 pltpu.SemaphoreType.DMA((rows,)),
-                pltpu.SemaphoreType.DMA((rows,)),
+                pltpu.SemaphoreType.DMA((rows, 2)),
             ],
             compiler_params=pltpu.CompilerParams(collective_id=0, has_side_effects=True,
-                                                 vmem_limit_bytes=60 * 1024 * 1024),
-        )(ao_rows, c_occ.T, c_vir)
+                                                 vmem_limit_bytes=44 * 1024 * 1024),
+        )(ao_rows, *(pltpu.with_memory_space_constraint(c, pltpu.HBM) for c in (c_occ.T, c_vir)))
+        v1, v2 = pl.pallas_call(
+            functools.partial(_unpack, n_occ, n_vir, keep),
+            out_shape=(jax.ShapeDtypeStruct((n_vir, n_occ, n_vir), F32),
+                       jax.ShapeDtypeStruct((n_occ, n_vir, n_vir), F32)),
+            in_specs=[pl.BlockSpec(memory_space=pltpu.VMEM)] * 2,
+            out_specs=(pl.BlockSpec(memory_space=pl.ANY), pl.BlockSpec(memory_space=pl.ANY)),
+            scratch_shapes=[pltpu.VMEM((n_occ, n_vir, n_vir), F32), pltpu.SemaphoreType.DMA((1 + n_occ // 8,))],
+            compiler_params=pltpu.CompilerParams(vmem_limit_bytes=8 * 1024 * 1024),
+        )(acc1, acc2)
         return v1.transpose(0, 2, 1), v2
 
     return jax.shard_map(local_part, mesh=mesh,

time: 81.7 us -> 75.2 us (0.920)
  the two profiles are of different devices: /device:TPU:103 before, /device:TPU:99 now
where the time goes in v4:
time: 75.2 us; the launch traced here: 75.1 us
  Pallas kernels  74.5 us (99%)
    pallas_call x1, Pallas kernels, local_part(): pl.pallas_call(functools.partial(_kernel, n_dev, rows, n_ao, n_occ, n_vir...  72.7 us
    pallas_call x1, Pallas kernels, local_part(): pl.pallas_call(functools.partial(_unpack, n_occ, n_vir, keep), out_shape=...  1.79 us

profile of v4, /device:TPU:99, one launch (start us, length us, event | category | flops | bytes accessed | tf_op | source)
XLA Modules:
  0.0 75.1 jit_solution(3731198452065530722)
XLA Ops:
  0.6 72.7 %shard_map.50 = (f32[104,32,104]{2,1,0:T(8,128)S(1)}, f32[32,112,128]{2,1,0:T(8,128)S(1)}) custom-call(bf16[5,160,160,160]{3,2,1,0:T(8,128)(2,1)} %a_hbm.1, bf16[32,160]{1,0:T(8,128)(2,1)} %bitcast.2, bf16[160,104]{1,0:T(8,128)(2,1)} %cv_hbm.1), custom_call_target="tpu_custom_call" | custom-call | tf_op jit(solution)/shard_map/pallas_call | solution.py:256
  73.3 1.8 %shard_map.51 = (f32[104,32,104]{2,1,0:T(8,128)}, f32[32,104,104]{2,1,0:T(8,128)}) custom-call(f32[104,32,104]{2,1,0:T(8,128)S(1)} %get-tuple-element.6.acc1, f32[32,112,128]{2,1,0:T(8,128)S(1)} %get-tuple-element.7.acc2), custom_call_target="tpu_custom_call" | custom-call | tf_op jit(solution)/shard_map/pallas_call | solution.py:286

commit v5 on v4

--- a/solution.py
+++ b/solution.py
@@ -1,4 +1,5 @@
 import functools
+import math
 
 import jax
 import jax.numpy as jnp
@@ -33,11 +34,37 @@
     return slots
 
 
+def _order(side):
+    def hops(d):
+        return min(d, side - d)
+
+    left = {(dx, dy) for dx in range(side) for dy in range(side)}
+    chips = []
+    for dx, dy in sorted(left, key=lambda c: (-(hops(c[0]) > 0) - (hops(c[1]) > 0),
+                                              abs(hops(c[0]) - hops(c[1])), hops(c[0]), c)):
+        for chip in ((dx, dy), (-dx % side, -dy % side), (dy, -dx % side), (-dy % side, dx)):
+            if chip in left:
+                left.remove(chip)
+                chips.append(chip)
+    return [(dx, dy, other) for dx, dy in chips for other in (1, 0)]
+
+
 def _kernel(n_dev, rows, n_ao, n_occ, n_vir, q_chunk, n_buf, pitch, keep, unroll,
             a_hbm, cot_hbm, cv_hbm, acc1, acc2,
             cot_ref, cv_ref, abuf, tb0, tb1, w2, ct, hov0, hov1, hoo0, hoo1, sb, rb, rep, wk, csem, asem, ssem, rsem):
     me = lax.axis_index('dev')
     hov, hoo = (hov0, hov1), (hoo0, hoo1)
+    side = math.isqrt(n_dev // 2)
+    core, cx, cy = lax.rem(me, 2), lax.rem(me // 2, side), me // (2 * side)
+    order = _order(side)
+
+    def partner(step, away):
+        dx, dy, other = order[step]
+        there = lax.rem(core + other, 2)
+        sign = away * (1 - 2 * (core if away > 0 else there))
+        return ((lax.rem(cy + dy * sign + side, side) * side + lax.rem(cx + dx * sign + side, side)) * 2
+                + there)
+
     n_chunk = n_ao // q_chunk
     n_half = n_dev // 2
     total = rows * n_chunk
@@ -83,7 +110,7 @@
         return pltpu.make_async_remote_copy(
             src_ref=sb.at[row, step], dst_ref=rb.at[row, step],
             send_sem=ssem.at[row], recv_sem=rsem.at[row, step // n_half],
-            device_id={'dev': lax.rem(me + 1 + step, n_dev)}, device_id_type=pl.DeviceIdType.MESH)
+            device_id={'dev': partner(step, 1)}, device_id_type=pl.DeviceIdType.MESH)
 
     @pl.loop(0, rows)
     def _(row):
@@ -103,13 +130,10 @@
             def _():
                 fetch(chunk + n_buf).start()
 
-        def owner_of(step):
-            return lax.rem(me + 1 + step, n_dev)
-
         def half(group):
             parts = []
             for u in range(unroll):
-                at = pl.ds(pl.multiple_of(owner_of(group * unroll + u) * pitch, 8), n_ao)
+                at = pl.ds(pl.multiple_of(partner(group * unroll + u, 1) * pitch, 8), n_ao)
                 parts.append(jnp.concatenate([tb0[at, :].astype(BF16), tb1[at, :].astype(BF16)], axis=1))
             h = _dot(jnp.concatenate(parts, axis=0), w2[...])
             for u in range(unroll):
@@ -150,8 +174,10 @@
 
     ident = (lax.broadcasted_iota(jnp.int32, (TILE, n_dev * TILE), 1) % TILE
              == lax.broadcasted_iota(jnp.int32, (TILE, n_dev * TILE), 0))
-    source = me - 1 - lax.broadcasted_iota(jnp.int32, (n_ao, n_dev * TILE), 1) // TILE
-    owner = jnp.where(source < 0, source + n_dev, source) * rows
+    slot = lax.broadcasted_iota(jnp.int32, (1, n_dev * TILE), 1) // TILE
+    owner = jnp.zeros_like(slot)
+    for step in range(n_dev):
+        owner = jnp.where(slot == step, partner(step, -1) * rows, owner)
     place = lax.broadcasted_iota(jnp.int32, (n_ao, n_dev * TILE), 0)
     n_tile = block_rows // TILE
     oo_rows = n_occ * TILE

time: 75.2 us -> 74.3 us (0.988)
  the two profiles are of different devices: /device:TPU:99 before, /device:TPU:97 now
where the time goes in v5:
time: 74.3 us; the launch traced here: 74.2 us
  Pallas kernels  73.6 us (99%)
    pallas_call x1, Pallas kernels, local_part(): pl.pallas_call(functools.partial(_kernel, n_dev, rows, n_ao, n_occ, n_vir...  71.8 us
    pallas_call x1, Pallas kernels, local_part(): pl.pallas_call(functools.partial(_unpack, n_occ, n_vir, keep), out_shape=...  1.79 us

profile of v5, /device:TPU:97, one launch (start us, length us, event | category | flops | bytes accessed | tf_op | source)
XLA Modules:
  0.0 74.2 jit_solution(11263362697627218810)
XLA Ops:
  0.6 71.8 %shard_map.50 = (f32[104,32,104]{2,1,0:T(8,128)S(1)}, f32[32,112,128]{2,1,0:T(8,128)S(1)}) custom-call(bf16[5,160,160,160]{3,2,1,0:T(8,128)(2,1)} %a_hbm.1, bf16[32,160]{1,0:T(8,128)(2,1)} %bitcast.2, bf16[160,104]{1,0:T(8,128)(2,1)} %cv_hbm.1), custom_call_target="tpu_custom_call" | custom-call | tf_op jit(solution)/shard_map/pallas_call | solution.py:282
  72.4 1.8 %shard_map.51 = (f32[104,32,104]{2,1,0:T(8,128)}, f32[32,104,104]{2,1,0:T(8,128)}) custom-call(f32[104,32,104]{2,1,0:T(8,128)S(1)} %get-tuple-element.6.acc1, f32[32,112,128]{2,1,0:T(8,128)S(1)} %get-tuple-element.7.acc2), custom_call_target="tpu_custom_call" | custom-call | tf_op jit(solution)/shard_map/pallas_call | solution.py:312

commit v6 on v5

--- a/solution.py
+++ b/solution.py
@@ -71,6 +71,7 @@
     moved = (n_occ + n_vir) // GROUP - keep
     slots = _pieces(n_vir, moved)
     block_rows = keep * GROUP
+    cuts = (0, 4 * TILE, block_rows)
 
     def fetch(chunk):
         slot = lax.rem(chunk, n_buf)
@@ -106,11 +107,13 @@
 
     pl.semaphore_wait(barrier, n_dev - 1)
 
-    def send(row, step):
-        return pltpu.make_async_remote_copy(
-            src_ref=sb.at[row, step], dst_ref=rb.at[row, step],
-            send_sem=ssem.at[row], recv_sem=rsem.at[row, step // n_half],
-            device_id={'dev': partner(step, 1)}, device_id_type=pl.DeviceIdType.MESH)
+    def send(row, steps):
+        for low, high in zip(cuts, cuts[1:]):
+            for step in steps:
+                pltpu.make_async_remote_copy(
+                    src_ref=sb.at[row, step, low:high], dst_ref=rb.at[row, step, low:high],
+                    send_sem=ssem.at[row], recv_sem=rsem.at[row, step // n_half],
+                    device_id={'dev': partner(step, 1)}, device_id_type=pl.DeviceIdType.MESH).start()
 
     @pl.loop(0, rows)
     def _(row):
@@ -167,10 +170,9 @@
                 half(group + 1)
             full(group)
             first, last = group * unroll, (group + 1) * unroll
-            for step in range(max(first - 2, 0), last - 2):
-                send(row, step).start()
+            send(row, range(max(first - 2, 0), last - 2))
         rb[row, n_dev - 1] = sb[row, n_dev - 1]
-        send(row, n_dev - 2).start()
+        send(row, [n_dev - 2])
 
     ident = (lax.broadcasted_iota(jnp.int32, (TILE, n_dev * TILE), 1) % TILE
              == lax.broadcasted_iota(jnp.int32, (TILE, n_dev * TILE), 0))

time: 74.3 us -> 73.3 us (0.987)
  Pallas kernels: 73.6 us -> 72.6 us
    pallas_call x1, Pallas kernels: 71.8 us -> 70.8 us  [local_part(): pl.pallas_call(functools.partial(_kernel, n_dev, rows, n_ao, n_occ, n_vir...]
where the time goes in v6:
time: 73.3 us
  Pallas kernels  72.6 us (99%)
    pallas_call x1, Pallas kernels, local_part(): pl.pallas_call(functools.partial(_kernel, n_dev, rows, n_ao, n_occ, n_vir...  70.8 us
    pallas_call x1, Pallas kernels, local_part(): pl.pallas_call(functools.partial(_unpack, n_occ, n_vir, keep), out_shape=...  1.79 us

profile of v6, /device:TPU:97, one launch (start us, length us, event | category | flops | bytes accessed | tf_op | source)
XLA Modules:
  0.0 73.3 jit_solution(14669011077948070965)
XLA Ops:
  0.6 70.8 %shard_map.50 = (f32[104,32,104]{2,1,0:T(8,128)S(1)}, f32[32,112,128]{2,1,0:T(8,128)S(1)}) custom-call(bf16[5,160,160,160]{3,2,1,0:T(8,128)(2,1)} %a_hbm.1, bf16[32,160]{1,0:T(8,128)(2,1)} %bitcast.2, bf16[160,104]{1,0:T(8,128)(2,1)} %cv_hbm.1), custom_call_target="tpu_custom_call" | custom-call | tf_op jit(solution)/shard_map/pallas_call | solution.py:284
  71.5 1.8 %shard_map.51 = (f32[104,32,104]{2,1,0:T(8,128)}, f32[32,104,104]{2,1,0:T(8,128)}) custom-call(f32[104,32,104]{2,1,0:T(8,128)S(1)} %get-tuple-element.6.acc1, f32[32,112,128]{2,1,0:T(8,128)S(1)} %get-tuple-element.7.acc2), custom_call_target="tpu_custom_call" | custom-call | tf_op jit(solution)/shard_map/pallas_call | solution.py:314

commit v7 on v6

--- a/solution.py
+++ b/solution.py
@@ -71,7 +71,7 @@
     moved = (n_occ + n_vir) // GROUP - keep
     slots = _pieces(n_vir, moved)
     block_rows = keep * GROUP
-    cuts = (0, 4 * TILE, block_rows)
+    cuts = (0, 2 * TILE, 4 * TILE, 6 * TILE, block_rows)
 
     def fetch(chunk):
         slot = lax.rem(chunk, n_buf)
@@ -218,13 +218,15 @@
         span = n_vir // n_block
         rhs = tiles(0, n_occ // TILE)
 
-        @pl.loop(0, n_block)
-        def _(block):
-            at = pl.ds(pl.multiple_of(oo_rows + block * (span * TILE), TILE), span * TILE)
+        def part(block):
+            at = pl.ds(oo_rows + block * (span * TILE), span * TILE)
             out = _dot(wk[at, cols], rhs)
             for c in range(n_occ // TILE):
                 acc1[pl.ds(block * span, span), c * TILE:(c + 1) * TILE, :] += (
                     out[:, c * LANES:c * LANES + n_vir].reshape(span, TILE, n_vir))
+
+        for block in range(n_block):
+            part(block)
 
     @pl.loop(0, rows - 1)
     def _(row):

time: 73.3 us -> 71.1 us (0.970)
  Pallas kernels: 72.6 us -> 70.4 us
    pallas_call x1, Pallas kernels: 70.8 us -> 68.6 us  [local_part(): pl.pallas_call(functools.partial(_kernel, n_dev, rows, n_ao, n_occ, n_vir...]
where the time goes in v7:
time: 71.1 us; the launch traced here: 71 us
  Pallas kernels  70.4 us (99%)
    pallas_call x1, Pallas kernels, local_part(): pl.pallas_call(functools.partial(_kernel, n_dev, rows, n_ao, n_occ, n_vir...  68.6 us
    pallas_call x1, Pallas kernels, local_part(): pl.pallas_call(functools.partial(_unpack, n_occ, n_vir, keep), out_shape=...  1.79 us

profile of v7, /device:TPU:97, one launch (start us, length us, event | category | flops | bytes accessed | tf_op | source)
XLA Modules:
  0.0 71.0 jit_solution(11350750382702750159)
XLA Ops:
  0.6 68.6 %shard_map.50 = (f32[104,32,104]{2,1,0:T(8,128)S(1)}, f32[32,112,128]{2,1,0:T(8,128)S(1)}) custom-call(bf16[5,160,160,160]{3,2,1,0:T(8,128)(2,1)} %a_hbm.1, bf16[32,160]{1,0:T(8,128)(2,1)} %bitcast.2, bf16[160,104]{1,0:T(8,128)(2,1)} %cv_hbm.1), custom_call_target="tpu_custom_call" | custom-call | tf_op jit(solution)/shard_map/pallas_call | solution.py:286
  69.2 1.8 %shard_map.51 = (f32[104,32,104]{2,1,0:T(8,128)}, f32[32,104,104]{2,1,0:T(8,128)}) custom-call(f32[104,32,104]{2,1,0:T(8,128)S(1)} %get-tuple-element.6.acc1, f32[32,112,128]{2,1,0:T(8,128)S(1)} %get-tuple-element.7.acc2), custom_call_target="tpu_custom_call" | custom-call | tf_op jit(solution)/shard_map/pallas_call | solution.py:316
